TPU v7x, 32 devices: a whole 2x2x4 slice. The times are simulated.
32 devices in a mesh: wl: 8 (over y, x, core), tile: 4 (over z).
Axes of the slice: x: 2, y: 2, z: 4, core: 2. Of those that a mesh axis runs over, the one named last changes fastest.
Arguments:
- forward: float32 [32, 2, 1024, 1024], P(('wl', 'tile')), may hold values from -6 to 6
- adjoint: float32 [32, 2, 1024, 1024], P(('wl', 'tile')), may hold values from -6 to 6
- mode: float32 [2, 1024], replicated, may hold values from -6 to 6
- target: float32 [32], P(('wl', 'tile')), may hold values from 0 to 2
- wl_index: int32 [32], P(('wl', 'tile')), may hold values from 0 to 31, each once
- tile_of: int32 [32], replicated, may hold values from 0 to 31, each once
- density: float32 [1024, 1024], P(('wl', 'tile')), may hold values from 0 to 1
Outputs:
- gradient: float32 [1024, 1024], P(('wl', 'tile'))
All inputs are finite; a program needn't handle non-finite values.
Results may differ from a plain program's by a relative error of at most 0.00002.
Values sent between devices are 32-bit elements; how exact they have to be, the bound alone decides.
A program may use at most 64 MiB of HBM per device.

v0:
```python
import functools

import jax
import jax.numpy as jnp
from jax import lax
from jax.experimental import pallas as pl
from jax.experimental.pallas import tpu as pltpu
from jax.sharding import PartitionSpec as P

MESH = pl.DeviceIdType.MESH
SUB = 8
LANES = 128
PIECES = 16
AHEAD = 3


def plane(wide):
    cores = 2 if wide % 2 == 0 else 1
    chips = wide // cores
    first = max(f for f in range(1, chips + 1) if chips % f == 0 and f * f <= chips)
    return first, chips // first, cores


def kernel(
    sizes, target_in, wl_in, tiles_in, mode_in, density_in, fwd, adj, shaped_hbm, norm_out,
    target, wl_index, tile_of, mode, density, shaped_out,
    line, f_src, f_recv, q_src, q_recv, slope, own, away, r0, r1, r2, r3,
    in_sem, side_sem, f_ssem, f_rsem, q_ssem, q_rsem, s0, e0, s1, e1, s2, e2, s3, e3, *bufs,
):
    g1, g2, cores, deep, groups, parts, rows, cols = sizes
    wide = g1 * g2 * cores
    devices = wide * deep
    tile_rows = rows // devices
    per_core = g1 * g2 * deep
    width = cols // parts
    f_bufs, a_bufs = bufs[:groups], bufs[groups:]
    w_me, z_me = lax.axis_index("wl"), lax.axis_index("tile")
    me = w_me * deep + z_me
    c_me = w_me % cores
    b_me = (w_me // cores) % g2
    a_me = w_me // (cores * g2)

    def at(a, b, c, z):
        return ((a * g2 + b) * cores + c, z)

    def everyone(o):
        f = (me + o) % devices
        return (f // deep, f % deep)

    barrier = pltpu.get_barrier_semaphore()

    @pl.loop(1, devices)
    def _(o):
        pl.semaphore_signal(barrier, inc=1, device_id=everyone(o), device_id_type=MESH)

    mon = rows // 2
    mt, mk, ms = mon // tile_rows, (mon % tile_rows) // SUB, mon % SUB
    line_copy = pltpu.make_async_copy(fwd.at[:, mt, mk], line, in_sem.at[2 * groups])
    mode_copy = pltpu.make_async_copy(mode_in, mode, side_sem.at[0])
    tile_copy = pltpu.make_async_copy(tiles_in, tile_of, side_sem.at[1])
    density_copy = pltpu.make_async_copy(density_in, density, side_sem.at[2])
    target_copy = pltpu.make_async_copy(target_in, target, side_sem.at[4])
    wl_copy = pltpu.make_async_copy(wl_in, wl_index, side_sem.at[5])
    for copy in (line_copy, mode_copy, tile_copy, density_copy, target_copy, wl_copy):
        copy.start()
    loads = []
    for k in range(groups):
        pair = (
            pltpu.make_async_copy(fwd.at[:, :, k], f_bufs[k], in_sem.at[2 * k]),
            pltpu.make_async_copy(adj.at[:, :, k], a_bufs[k], in_sem.at[2 * k + 1]),
        )
        if k == 0:
            for copy in pair:
                copy.start()
        loads.append(pair)

    line_copy.wait()
    mode_copy.wait()
    re, im = line[0, ms : ms + 1, :], line[1, ms : ms + 1, :]
    m_re, m_im = mode[0:1, :], mode[1:2, :]
    over_re = jnp.sum(re * m_re - im * m_im, axis=1, keepdims=True)
    over_im = jnp.sum(re * m_im + im * m_re, axis=1, keepdims=True)
    fom = jnp.broadcast_to((over_re * over_re + over_im * over_im) / cols, (1, LANES))
    f_src[...] = fom

    pl.semaphore_wait(barrier, devices - 1)

    def share(src, recv, ssem, rsem):
        def copy(o):
            return pltpu.make_async_remote_copy(
                src_ref=src, dst_ref=recv.at[o - 1],
                send_sem=ssem.at[o - 1], recv_sem=rsem.at[o - 1],
                device_id=everyone(o), device_id_type=MESH,
            )

        @pl.loop(1, devices)
        def _(o):
            copy(o).start()

        return copy

    f_copy = share(f_src, f_recv, f_ssem, f_rsem)
    for pair in loads[1:]:
        for copy in pair:
            copy.start()
    density_copy.wait()
    slope[...] = 4.0 * (1.0 - jnp.tanh(4.0 * (density[...] - 0.5)) ** 2)

    def finish(copy):
        @pl.loop(1, devices)
        def _(o):
            copy(o).wait()

    finish(f_copy)
    total_fom = fom + jnp.sum(f_recv[...], axis=0)
    scale = total_fom / devices + 1.0
    target_copy.wait()
    wl_copy.wait()
    weight = target[0] - fom / scale
    freq = 1.0 + wl_index[0].astype(jnp.float32) / devices
    factor = jnp.concatenate([weight * freq * freq] * (width // LANES), axis=1)
    factor = jnp.broadcast_to(factor, (SUB, width))
    tile_copy.wait()

    def order(piece):
        return (g1, g2) if piece % 2 == 0 else (g2, g1)

    def build(k):
        for copy in loads[k]:
            copy.wait()
        for half in range(cores):

            @pl.loop(0, g1 * g2)
            def _(i):
                hi, lo = i // g2, i % g2
                c = (c_me + half) % cores
                base = ((((a_me + hi) % g1) * g2 + (b_me + lo) % g2) * cores + c) * deep
                slots = (i * deep, (lo * g1 + hi) * deep)
                for oz in range(deep):
                    t = tile_of[base + (z_me + oz) % deep]
                    for p in range(parts):
                        cs = slice(p * width, (p + 1) * width)
                        piece = k * parts + p
                        (away if half else own)[piece, slots[piece % 2] + oz] = factor * (
                            f_bufs[k][0, t, :, cs] * a_bufs[k][0, t, :, cs]
                            - f_bufs[k][1, t, :, cs] * a_bufs[k][1, t, :, cs]
                        )

    def swap(piece):
        return pltpu.make_async_remote_copy(
            src_ref=away.at[piece], dst_ref=r0.at[piece],
            send_sem=s0.at[piece], recv_sem=e0.at[piece],
            device_id=at(a_me, b_me, (c_me + 1) % cores, z_me), device_id_type=MESH,
        )

    def scatter(piece, step):
        n1, n2 = order(piece)
        n = (n1, n2, deep)[step]
        span = (n2 * deep, deep, 1)[step]
        recv, ssem, rsem = ((r1, s1, e1), (r2, s2, e2), (r3, s3, e3))[step]
        axis = step if step == 2 else (step + piece) % 2
        copies = []
        for o in range(1, n):
            where = (
                at((a_me + o) % g1, b_me, c_me, z_me) if axis == 0
                else at(a_me, (b_me + o) % g2, c_me, z_me) if axis == 1
                else at(a_me, b_me, c_me, (z_me + o) % deep)
            )
            copies.append(pltpu.make_async_remote_copy(
                src_ref=own.at[piece, pl.ds(o * span, span)],
                dst_ref=recv.at[piece, pl.ds((o - 1) * span, span)],
                send_sem=ssem.at[piece, o - 1], recv_sem=rsem.at[piece, o - 1],
                device_id=where, device_id_type=MESH,
            ))
        return copies, recv, span, n

    def start(piece, step):
        for copy in scatter(piece, step)[0]:
            copy.start()

    def add(piece, step):
        copies, recv, span, n = scatter(piece, step)
        for copy in copies:
            copy.wait_recv()

        value = own[piece, :span]
        for o in range(n - 1):
            value = value + recv[piece, o * span : (o + 1) * span]
        own[piece, :span] = value

    pieces = groups * parts

    def first(piece):
        if cores > 1:
            swap(piece).wait_recv()
            own[piece] = own[piece] + r0[piece]

        start(piece, 0)

    built = 0

    def make(upto):
        nonlocal built
        while built < min(upto, groups):
            build(built)
            if cores > 1:
                for p in range(parts):
                    swap(built * parts + p).start()
            built += 1

    def open_pair(pair):
        make((2 * pair + 1) // parts + 2)
        for piece in (2 * pair, 2 * pair + 1):
            first(piece)

    for turn in range(pieces // 2 + 1):
        if turn == 0:
            for pair in range(min(AHEAD, pieces // 2)):
                open_pair(pair)
        if turn < pieces // 2:
            for piece in (2 * turn, 2 * turn + 1):
                add(piece, 0)
                start(piece, 1)
            if turn + AHEAD < pieces // 2:
                open_pair(turn + AHEAD)
        if 1 <= turn <= pieces // 2:
            for piece in (2 * turn - 2, 2 * turn - 1):
                add(piece, 1)
                start(piece, 2)

    squares = jnp.zeros((1, 1), jnp.float32)
    for piece in range(pieces):
        copies, recv, span, n = scatter(piece, 2)
        for copy in copies:
            copy.wait_recv()
        value = own[piece, 0]
        for o in range(n - 1):
            value = value + recv[piece, o]
        k, p = piece // parts, piece % parts
        rs, cs = slice(k * SUB, (k + 1) * SUB), slice(p * width, (p + 1) * width)
        shaped = value * slope[rs, cs]
        shaped_out[rs, cs] = shaped
        squares = squares + jnp.sum(shaped * shaped, keepdims=True)
    out_copy = pltpu.make_async_copy(shaped_out, shaped_hbm, side_sem.at[3])
    out_copy.start()
    mine = jnp.broadcast_to(squares, (1, LANES))
    q_src[...] = mine
    q_copy = share(q_src, q_recv, q_ssem, q_rsem)

    for piece in range(pieces):
        if cores > 1:
            swap(piece).wait_send()
        for step in range(3):
            for copy in scatter(piece, step)[0]:
                copy.wait_send()
    out_copy.wait()
    finish(q_copy)
    squares = mine + jnp.sum(q_recv[...], axis=0)
    norm_out[...] = jnp.sqrt(squares / (rows * cols) + 1e-06)


def per_device(forward, adjoint, mode, target, wl_index, tile_of, density):
    wide, deep = lax.axis_size("wl"), lax.axis_size("tile")
    devices = wide * deep
    rows, cols = forward.shape[2:]
    g1, g2, cores = plane(wide)
    tile_rows = rows // devices
    groups = tile_rows // SUB
    parts = max(1, min(PIECES // groups, cols // LANES))
    pieces = groups * parts
    width = cols // parts
    per_core = g1 * g2 * deep
    fwd = forward.reshape(2, devices, groups, SUB, cols)
    adj = adjoint.reshape(2, devices, groups, SUB, cols)
    f32 = jnp.float32
    dma = pltpu.SemaphoreType.DMA
    most = max(g1, g2, 2) - 1
    block = lambda n: pltpu.VMEM((pieces, max(n, 1), SUB, width), f32)
    sizes = (g1, g2, cores, deep, groups, parts, rows, cols)
    peers = max(devices - 1, 1)
    vmem = pl.BlockSpec(memory_space=pltpu.VMEM)
    hbm = pl.BlockSpec(memory_space=pl.ANY)
    third = max(deep - 1, 1)
    shaped, norm = pl.pallas_call(
        functools.partial(kernel, sizes),
        out_shape=(
            jax.ShapeDtypeStruct((tile_rows, cols), f32),
            jax.ShapeDtypeStruct((1, LANES), f32),
        ),
        in_specs=[hbm, hbm, hbm, hbm, hbm, hbm, hbm],
        out_specs=(hbm, vmem),
        scratch_shapes=[
            pltpu.SMEM((1,), f32),
            pltpu.SMEM((1,), jnp.int32),
            pltpu.SMEM((devices,), jnp.int32),
            pltpu.VMEM(mode.shape, f32),
            pltpu.VMEM((tile_rows, cols), f32),
            pltpu.VMEM((tile_rows, cols), f32),
            pltpu.VMEM((2, SUB, cols), f32),
            pltpu.VMEM((1, LANES), f32),
            pltpu.VMEM((peers, 1, LANES), f32),
            pltpu.VMEM((1, LANES), f32),
            pltpu.VMEM((peers, 1, LANES), f32),
            pltpu.VMEM((tile_rows, cols), f32),
            block(per_core),
            block(per_core),
            block(per_core),
            block(per_core),
            block(per_core // min(g1, g2)),
            block(third),
            dma((2 * groups + 1,)),
            dma((6,)),
            dma((peers,)), dma((peers,)), dma((peers,)), dma((peers,)),
            dma((pieces,)), dma((pieces,)),
            dma((pieces, most)), dma((pieces, most)),
            dma((pieces, most)), dma((pieces, most)),
            dma((pieces, third)), dma((pieces, third)),
        ]
        + [pltpu.VMEM((2, devices, SUB, cols), f32)] * (2 * groups),
        compiler_params=pltpu.CompilerParams(
            collective_id=0, has_side_effects=True, vmem_limit_bytes=60 * 2**20
        ),
        name="assemble",
    )(target, wl_index, tile_of, mode, density, fwd, adj)
    return shaped / norm[0, 0]


def solution(mesh):
    in_specs = (
        P(("wl", "tile"), None, None, None),
        P(("wl", "tile"), None, None, None),
        P(),
        P(("wl", "tile")),
        P(("wl", "tile")),
        P(),
        P(("wl", "tile"), None),
    )
    out_specs = P(("wl", "tile"), None)
    return jax.shard_map(
        per_device, mesh=mesh, in_specs=in_specs, out_specs=out_specs, check_vma=False
    )
```

profile of v0, /device:TPU:0, one launch (start us, length us, event | category | flops | bytes accessed | tf_op | source)
XLA Modules:
  0.0 48.7 jit_solution(17390782901054415673)
XLA Ops:
  1.3 45.1 %assemble.1 = (f32[32,1024]{1,0:T(8,128)}, f32[1,128]{1,0:T(1,128)}) custom-call(f32[1]{0:T(128)S(6)} %copy.8.target_in, s32[1]{0:T(128)S(6)} %copy.9.wl_in, s32[32]{0:T(128)} %tiles_in.1, f32[2,1024]{1,0:T(2,128)} %mode_in.1, f32[32,1024]{1,0:T(8,128)} %density_in.1, f32[2,32,4,8,1024]{4,3,2,1,0:T(8,128)} %bitcast.4, f32[2,32,4,8,1024]{4,3,2,1,0:T(8,128)} %bitcast.5), custom_call_target="tpu_custom_call" | custom-call | tf_op jit(solution)/shard_map/assemble/pallas_call | solution.py:284
  46.4 2.3 %broadcast_divide_fusion = f32[32,1024]{1,0:T(8,128)} fusion(f32[32,1024]{1,0:T(8,128)} %get-tuple-element.7, f32[]{:T(128)} %bitcast.6), kind=kLoop, calls=%fused_computation | loop fusion | flops 32768 | bytes 262148 | tf_op jit(solution)/shard_map/div | solution.py:325
where the time goes:
time: 48.8 us; the launch traced here: 48.7 us
  Pallas kernels  45.1 us (92%)
  other arithmetic  2.26 us (5%)
  between operations  1.3 us (3%)
    pallas_call x1, Pallas kernels, per_device(): pl.pallas_call(functools.partial(kernel, sizes), out_shape=(jax.ShapeDtyp...  45.1 us
    div x1, other arithmetic, per_device(): return shaped / norm[0, 0]  2.26 us

commit v1 on v0

v1 whole, which is shorter than its diff:
```python
import functools

import jax
import jax.numpy as jnp
from jax import lax
from jax.experimental import pallas as pl
from jax.experimental.pallas import tpu as pltpu
from jax.sharding import PartitionSpec as P

MESH = pl.DeviceIdType.MESH
SUB = 8
LANES = 128
PIECES = 16
PATTERNS = ("AzBw", "BzAw")
SPACE = 0.3
LAG = 4.0
EARLY = 16
ORDER = ()


def plane(wide):
    cores = 2 if wide % 2 == 0 else 1
    chips = wide // cores
    first = max(f for f in range(1, chips + 1) if chips % f == 0 and f * f <= chips)
    return first, chips // first, cores


def digits_of(axis, size):
    out, stride, f = [], 1, 2
    while stride < size:
        while (size // stride) % f:
            f += 1
        out.append((axis, f, stride))
        stride *= f
    return out


def radix(step):
    n = 1
    for d in step:
        n *= d[1]
    return n


def steps_of(pattern, dims):
    parts = {"A": dims[0], "B": dims[1], "Z": dims[2], "z": dims[2][:1], "w": dims[2][1:]}
    return [tuple(parts[c]) for c in pattern if parts[c]]


def schedule(orders):
    ops = []
    if sorted(ORDER) == [(i, s) for i, steps in enumerate(orders) for s in range(-1, len(steps))]:
        return ORDER
    for i, steps in enumerate(orders):
        ops.append((i * SPACE, i, -1))
        for s in range(len(steps)):
            ops.append((i * SPACE + (s + 1) * LAG, i, s))
    return [(i, s) for _, i, s in sorted(ops)]


def kernel(
    sizes, orders, target, wl_index, tiles_in, mode_in, density_in, fwd, adj, shaped_out, norm_out,
    tile_of, mode, density, line, f_src, f_recv, w_src, w_recv, q_src, q_recv, slope, own, away, r0, recv,
    in_sem, side_sem, pair_sem, swap_sem, step_sem, *bufs,
):
    g1, g2, cores, deep, groups, parts, rows, cols = sizes
    devices = g1 * g2 * cores * deep
    tile_rows = rows // devices
    per_core = g1 * g2 * deep
    width = cols // parts
    pieces = groups * parts
    f_bufs, a_bufs = bufs[:groups], bufs[groups:]
    w_me, z_me = lax.axis_index("wl"), lax.axis_index("tile")
    c_me = w_me % cores
    me = (w_me // (cores * g2), (w_me // cores) % g2, z_me, c_me)
    dims = [digits_of(0, g1), digits_of(1, g2), digits_of(2, deep), digits_of(3, cores)]

    def shift(coords, digit, o):
        axis, f, stride = digit
        d = (coords[axis] // stride) % f
        moved = coords[axis] + ((d + o) % f - d) * stride
        return coords[:axis] + (moved,) + coords[axis + 1 :]

    def split(digits, index):
        out = []
        for d in digits:
            out.append(index % d[1])
            index = index // d[1]
        return out

    def at(coords):
        a, b, z, c = coords
        return ((a * g2 + b) * cores + c, z)

    def flat(coords):
        w, z = at(coords)
        return w * deep + z

    def move(digits, index):
        coords = me
        for d, o in zip(digits, split(digits, index)):
            if not isinstance(o, int) or o:
                coords = shift(coords, d, o)
        return coords

    every = [d for axis in dims for d in axis]
    far = lambda j: -sum(d[2] * (d[0] != 3) + 0.5 for d, o in zip(every, split(every, j)) if o)
    others = sorted(range(1, devices), key=far)
    other = {j: at(move(every, j)) for j in others}

    barrier = pltpu.get_barrier_semaphore()
    for j in others:
        pl.semaphore_signal(barrier, inc=1, device_id=other[j], device_id_type=MESH)

    mon = rows // 2
    mt, mk, ms = mon // tile_rows, (mon % tile_rows) // SUB, mon % SUB
    line_copy = pltpu.make_async_copy(fwd.at[:, mt, mk], line, in_sem.at[2 * groups])
    mode_copy = pltpu.make_async_copy(mode_in, mode, side_sem.at[0])
    tile_copy = pltpu.make_async_copy(tiles_in, tile_of, side_sem.at[1])
    density_copy = pltpu.make_async_copy(density_in, density, side_sem.at[2])
    for copy in (line_copy, mode_copy, tile_copy):
        copy.start()
    loads = []
    for k in range(groups):
        pair = (
            pltpu.make_async_copy(fwd.at[:, :, k], f_bufs[k], in_sem.at[2 * k]),
            pltpu.make_async_copy(adj.at[:, :, k], a_bufs[k], in_sem.at[2 * k + 1]),
        )
        loads.append(pair)
    for copy in loads[0]:
        copy.start()

    line_copy.wait()
    mode_copy.wait()
    for pair in loads[1:]:
        for copy in pair:
            copy.start()
    density_copy.start()
    re, im = line[0, ms : ms + 1, :], line[1, ms : ms + 1, :]
    m_re, m_im = mode[0:1, :], mode[1:2, :]
    over_re = jnp.sum(re * m_re - im * m_im, axis=1, keepdims=True)
    over_im = jnp.sum(re * m_im + im * m_re, axis=1, keepdims=True)
    fom = jnp.broadcast_to((over_re * over_re + over_im * over_im) / cols, (1, LANES))
    f_src[...] = fom
    freq = 1.0 + wl_index[0].astype(jnp.float32) / devices
    aim, part = target[0] * (freq * freq), fom * (freq * freq)
    w_src[0:1, :] = jnp.full((1, LANES), aim)
    w_src[1:2, :] = part

    pl.semaphore_wait(barrier, devices - 1)

    def share(src, dst, sems):
        for j in others:
            pltpu.make_async_remote_copy(
                src_ref=src, dst_ref=dst.at[j - 1], send_sem=side_sem.at[sems], recv_sem=side_sem.at[sems + 1],
                device_id=other[j], device_id_type=MESH,
            ).start()
        return pltpu.make_async_remote_copy(
            src_ref=dst, dst_ref=dst, send_sem=side_sem.at[sems], recv_sem=side_sem.at[sems + 1],
            device_id=other[others[0]], device_id_type=MESH,
        )

    f_copy = share(f_src, f_recv, 3)
    partner = at(move(dims[3], 1)) if cores > 1 else None

    def swap_of(src, dst, ssem, rsem):
        return pltpu.make_async_remote_copy(
            src_ref=src, dst_ref=dst, send_sem=ssem, recv_sem=rsem, device_id=partner, device_id_type=MESH
        )

    if cores > 1:
        w_copy = swap_of(w_src, w_recv, pair_sem.at[0], pair_sem.at[1])
        w_copy.start()

    flat_dims = dims[0] + dims[1] + dims[2]
    weights = []
    for steps in orders:
        weight, span = {}, per_core
        for step in steps:
            span //= radix(step)
            unit = span
            for d in step:
                weight[d] = unit
                unit *= d[1]
        weights.append(weight)
    kinds = sorted({tuple(w[d] for d in flat_dims) for w in weights})
    kind_of = [kinds.index(tuple(w[d] for d in flat_dims)) for w in weights]
    wide_dims = dims[0] + dims[1]

    tile_copy.wait()

    def build(k):
        for copy in loads[k]:
            copy.wait()
        for half in range(cores):

            @pl.loop(0, g1 * g2)
            def _(i):
                offs = split(wide_dims, i)
                coords = me
                for d, o in zip(wide_dims, offs):
                    coords = shift(coords, d, o)
                if half:
                    coords = shift(coords, dims[3][0], half)
                base = [sum(o * kind[n] for n, o in enumerate(offs)) for kind in kinds]
                for oz in range(deep):
                    zo = split(dims[2], oz)
                    there = coords
                    for d, o in zip(dims[2], zo):
                        if o:
                            there = shift(there, d, o)
                    t = tile_of[flat(there)]
                    for p in range(parts):
                        cs = slice(p * width, (p + 1) * width)
                        piece = k * parts + p
                        kind = kind_of[piece]
                        slot = base[kind] + sum(o * kinds[kind][len(wide_dims) + n] for n, o in enumerate(zo))
                        (away if half else own)[piece, slot] = (
                            f_bufs[k][0, t, :, cs] * a_bufs[k][0, t, :, cs]
                            - f_bufs[k][1, t, :, cs] * a_bufs[k][1, t, :, cs]
                        )

    def swap(piece):
        return swap_of(away.at[piece], r0.at[piece], pair_sem.at[2], swap_sem.at[piece])

    for k in range(groups):
        build(k)
        for piece in range(k * parts, (k + 1) * parts):
            if cores > 1 and piece < EARLY:
                swap(piece).start()

    density_copy.wait()
    slope[...] = 4.0 * (1.0 - jnp.tanh(4.0 * (density[...] - 0.5)) ** 2)

    f_copy.wait_recv()
    for piece in range(EARLY, pieces):
        if cores > 1:
            swap(piece).start()
    total_fom = fom + jnp.sum(f_recv[...], axis=0)
    scale = total_fom / devices + 1.0

    def wide_factor(a, b):
        return jnp.broadcast_to(jnp.concatenate([a - b / scale] * (width // LANES), axis=1), (SUB, width))

    factor = wide_factor(aim, part)
    if cores > 1:
        w_copy.wait_recv()
        other_factor = wide_factor(w_recv[0:1, :], w_recv[1:2, :])

    spans, bases = [], []
    for steps in orders:
        span, base, ss, bs = per_core, 0, [], []
        for step in steps:
            span //= radix(step)
            ss.append(span)
            bs.append(base)
            base += (radix(step) - 1) * span
        spans.append(ss)
        bases.append(bs)

    def start(piece, s):
        step, span, base = orders[piece][s], spans[piece][s], bases[piece][s]
        for j in range(1, radix(step)):
            pltpu.make_async_remote_copy(
                src_ref=own.at[piece, pl.ds(j * span, span)],
                dst_ref=recv.at[piece, pl.ds(base + (j - 1) * span, span)],
                send_sem=pair_sem.at[3], recv_sem=step_sem.at[piece, s],
                device_id=at(move(step, j)), device_id_type=MESH,
            ).start()

    def take(piece, s):
        step, span, base = orders[piece][s], spans[piece][s], bases[piece][s]
        got = recv.at[piece, pl.ds(base, (radix(step) - 1) * span)]
        pltpu.make_async_remote_copy(
            src_ref=got, dst_ref=got, send_sem=pair_sem.at[3], recv_sem=step_sem.at[piece, s],
            device_id=at(move(step, 1)), device_id_type=MESH,
        ).wait_recv()
        value = own[piece, :span]
        for j in range(radix(step) - 1):
            value = value + recv[piece, base + j * span : base + (j + 1) * span]
        return value

    squares = jnp.zeros((SUB, LANES), jnp.float32)
    for piece, s in schedule(orders):
        steps = orders[piece]
        if s < 0:
            if cores > 1:
                swap(piece).wait_recv()
                own[piece] = own[piece] * factor + r0[piece] * other_factor
            else:
                own[piece] = own[piece] * factor
            if steps:
                start(piece, 0)
        elif s < len(steps) - 1:
            own[piece, : spans[piece][s]] = take(piece, s)
            start(piece, s + 1)
        if s == len(steps) - 1:
            value = take(piece, s)[0] if steps else own[piece, 0]
            k, p = piece // parts, piece % parts
            rs, cs = slice(k * SUB, (k + 1) * SUB), slice(p * width, (p + 1) * width)
            shaped = value * slope[rs, cs]
            shaped_out[rs, cs] = shaped
            shaped = shaped * shaped
            for n in range(width // LANES):
                squares = squares + shaped[:, n * LANES : (n + 1) * LANES]
    mine = jnp.sum(squares, axis=0, keepdims=True)
    q_src[...] = mine
    q_copy = share(q_src, q_recv, 5)

    if cores > 1:
        w_copy.wait_send()
        swap_of(away, r0, pair_sem.at[2], pair_sem.at[2]).wait_send()
    if per_core > 1:
        sent = own.at[:, pl.ds(0, per_core - 1)]
        pltpu.make_async_remote_copy(
            src_ref=sent, dst_ref=sent, send_sem=pair_sem.at[3], recv_sem=pair_sem.at[3],
            device_id=other[others[0]], device_id_type=MESH,
        ).wait_send()
    f_copy.wait_send()
    q_copy.wait_recv()
    squares = jnp.sum(mine + jnp.sum(q_recv[...], axis=0), axis=1, keepdims=True)
    norm_out[...] = jnp.broadcast_to(jnp.sqrt(squares / (rows * cols) + 1e-06), (1, LANES))
    q_copy.wait_send()


def per_device(forward, adjoint, mode, target, wl_index, tile_of, density):
    wide, deep = lax.axis_size("wl"), lax.axis_size("tile")
    devices = wide * deep
    rows, cols = forward.shape[2:]
    g1, g2, cores = plane(wide)
    tile_rows = rows // devices
    groups = tile_rows // SUB
    parts = max(1, min(PIECES // groups, cols // LANES))
    pieces = groups * parts
    width = cols // parts
    per_core = g1 * g2 * deep
    dims = [digits_of(0, g1), digits_of(1, g2), digits_of(2, deep)]
    orders = [steps_of(PATTERNS[i % len(PATTERNS)], dims) for i in range(pieces)]
    fwd = forward.reshape(2, devices, groups, SUB, cols)
    adj = adjoint.reshape(2, devices, groups, SUB, cols)
    f32 = jnp.float32
    dma = pltpu.SemaphoreType.DMA
    block = lambda n: pltpu.VMEM((pieces, n, SUB, width), f32)
    sizes = (g1, g2, cores, deep, groups, parts, rows, cols)
    peers = max(devices - 1, 1)
    vmem = pl.BlockSpec(memory_space=pltpu.VMEM)
    smem = pl.BlockSpec(memory_space=pltpu.SMEM)
    hbm = pl.BlockSpec(memory_space=pl.ANY)
    shaped, norm = pl.pallas_call(
        functools.partial(kernel, sizes, orders),
        out_shape=(pltpu.VMEM((tile_rows, cols), f32), pltpu.VMEM((1, LANES), f32)),
        in_specs=[smem, smem, hbm, hbm, hbm, hbm, hbm],
        out_specs=(vmem, vmem),
        scratch_shapes=[
            pltpu.SMEM((devices,), jnp.int32),
            pltpu.VMEM(mode.shape, f32),
            pltpu.VMEM((tile_rows, cols), f32),
            pltpu.VMEM((2, SUB, cols), f32),
            pltpu.VMEM((1, LANES), f32),
            pltpu.VMEM((peers, 1, LANES), f32),
            pltpu.VMEM((2, LANES), f32),
            pltpu.VMEM((2, LANES), f32),
            pltpu.VMEM((1, LANES), f32),
            pltpu.VMEM((peers, 1, LANES), f32),
            pltpu.VMEM((tile_rows, cols), f32),
            block(per_core),
            block(per_core),
            block(per_core),
            block(per_core),
            dma((2 * groups + 1,)),
            dma((7,)),
            dma((4,)),
            dma((pieces,)),
            dma((pieces, max(len(o) for o in orders))),
        ]
        + [pltpu.VMEM((2, devices, SUB, cols), f32)] * (2 * groups),
        compiler_params=pltpu.CompilerParams(
            collective_id=0, has_side_effects=True, vmem_limit_bytes=60 * 2**20
        ),
        name="assemble",
    )(target, wl_index, tile_of, mode, density, fwd, adj)
    return shaped / norm[0, 0]


def solution(mesh):
    in_specs = (
        P(("wl", "tile"), None, None, None),
        P(("wl", "tile"), None, None, None),
        P(),
        P(("wl", "tile")),
        P(("wl", "tile")),
        P(),
        P(("wl", "tile"), None),
    )
    out_specs = P(("wl", "tile"), None)
    return jax.shard_map(
        per_device, mesh=mesh, in_specs=in_specs, out_specs=out_specs, check_vma=False
    )
```

time: 48.8 us -> 40.9 us (0.84)
  Pallas kernels: 45.1 us -> 38.7 us
  other arithmetic: 2.26 us -> 0.7 us
    pallas_call x1, Pallas kernels: 45.1 us -> 38.7 us  [per_device(): pl.pallas_call(functools.partial(kernel, sizes, orders), out_shape=(pltpu...]
    div x1, other arithmetic: 2.26 us -> 0.7 us  [per_device(): return shaped / norm[0, 0]]
where the time goes in v1:
time: 40.9 us; the launch traced here: 40.7 us
  Pallas kernels  38.7 us (95%)
  between operations  1.3 us (3%)
  other arithmetic  0.7 us (2%)
    pallas_call x1, Pallas kernels, per_device(): pl.pallas_call(functools.partial(kernel, sizes, orders), out_shape=(pltpu...  38.7 us

profile of v1, /device:TPU:0, one launch (start us, length us, event | category | flops | bytes accessed | tf_op | source)
XLA Modules:
  0.0 40.7 jit_solution(12062962129462711259)
XLA Ops:
  1.3 38.7 %assemble.1 = (f32[32,1024]{1,0:T(8,128)S(1)}, f32[1,128]{1,0:T(1,128)S(1)}) custom-call(f32[1]{0:T(128)S(6)} %copy.8.target, s32[1]{0:T(128)S(6)} %copy.9.wl_index, s32[32]{0:T(128)} %tiles_in.1, f32[2,1024]{1,0:T(2,128)} %mode_in.1, f32[32,1024]{1,0:T(8,128)} %density_in.1, f32[2,32,4,8,1024]{4,3,2,1,0:T(8,128)} %bitcast.5, f32[2,32,4,8,1024]{4,3,2,1,0:T(8,128)} %bitcast.6), custom_call_target="tpu_custom_call" | custom-call | tf_op jit(solution)/shard_map/assemble/pallas_call | solution.py:349
  40.0 0.7 %broadcast_divide_fusion = f32[32,1024]{1,0:T(8,128)} fusion(f32[32,1024]{1,0:T(8,128)S(1)} %get-tuple-element.7, f32[]{:T(128)S(1)} %bitcast.4), kind=kLoop, calls=%fused_computation | loop fusion | flops 32768 | bytes 262148 | tf_op jit(solution)/shard_map/div | solution.py:382

commit v2 on v1

--- a/solution.py
+++ b/solution.py
@@ -11,11 +11,14 @@
 SUB = 8
 LANES = 128
 PIECES = 16
-PATTERNS = ("AzBw", "BzAw")
+PATTERNS = ('B.z.w.A', 'A.B.zw', 'w.A.z.B', 'B.w.A.z', 'A.z.B.w', 'A.B.w.z', 'A.w.z.B', 'A.B.zw', 'z.A.B.w', 'B.A.z.w', 'B.z.A.w', 'z.B.A.w', 'B.w.A.z', 'w.A.B.z', 'A.B.zw', 'B.A.zw')
 SPACE = 0.3
 LAG = 4.0
 EARLY = 16
-ORDER = ()
+PRE = 0
+DELAY = 2000
+FIRST = 1
+ORDER = ((0, -1), (1, -1), (2, -1), (3, -1), (4, -1), (5, -1), (6, -1), (7, -1), (8, -1), (9, -1), (10, -1), (11, -1), (12, -1), (13, -1), (14, -1), (15, -1), (0, 0), (1, 0), (2, 0), (3, 0), (4, 0), (5, 0), (6, 0), (7, 0), (8, 0), (9, 0), (10, 0), (11, 0), (12, 0), (13, 0), (14, 0), (15, 0), (0, 1), (1, 1), (2, 1), (3, 1), (4, 1), (5, 1), (6, 1), (7, 1), (8, 1), (9, 1), (10, 1), (11, 1), (12, 1), (13, 1), (14, 1), (15, 1), (0, 2), (1, 2), (2, 2), (3, 2), (4, 2), (5, 2), (6, 2), (8, 2), (9, 2), (10, 2), (11, 2), (12, 2), (13, 2), (0, 3), (2, 3), (3, 3), (4, 3), (12, 3), (13, 3), (6, 3), (8, 3), (7, 2), (9, 3), (5, 3), (14, 2), (15, 2), (10, 3), (11, 3))
 
 
 def plane(wide):
@@ -43,8 +46,9 @@
 
 
 def steps_of(pattern, dims):
-    parts = {"A": dims[0], "B": dims[1], "Z": dims[2], "z": dims[2][:1], "w": dims[2][1:]}
-    return [tuple(parts[c]) for c in pattern if parts[c]]
+    parts = {"A": dims[0], "B": dims[1], "z": dims[2][:1], "w": dims[2][1:]}
+    steps = [tuple(d for c in step for d in parts[c]) for step in pattern.split(".")]
+    return [step for step in steps if step]
 
 
 def schedule(orders):
@@ -127,12 +131,13 @@
             pltpu.make_async_copy(adj.at[:, :, k], a_bufs[k], in_sem.at[2 * k + 1]),
         )
         loads.append(pair)
-    for copy in loads[0]:
-        copy.start()
+    for pair in loads[:FIRST]:
+        for copy in pair:
+            copy.start()
 
     line_copy.wait()
     mode_copy.wait()
-    for pair in loads[1:]:
+    for pair in loads[FIRST:]:
         for copy in pair:
             copy.start()
     density_copy.start()
@@ -146,31 +151,6 @@
     aim, part = target[0] * (freq * freq), fom * (freq * freq)
     w_src[0:1, :] = jnp.full((1, LANES), aim)
     w_src[1:2, :] = part
-
-    pl.semaphore_wait(barrier, devices - 1)
-
-    def share(src, dst, sems):
-        for j in others:
-            pltpu.make_async_remote_copy(
-                src_ref=src, dst_ref=dst.at[j - 1], send_sem=side_sem.at[sems], recv_sem=side_sem.at[sems + 1],
-                device_id=other[j], device_id_type=MESH,
-            ).start()
-        return pltpu.make_async_remote_copy(
-            src_ref=dst, dst_ref=dst, send_sem=side_sem.at[sems], recv_sem=side_sem.at[sems + 1],
-            device_id=other[others[0]], device_id_type=MESH,
-        )
-
-    f_copy = share(f_src, f_recv, 3)
-    partner = at(move(dims[3], 1)) if cores > 1 else None
-
-    def swap_of(src, dst, ssem, rsem):
-        return pltpu.make_async_remote_copy(
-            src_ref=src, dst_ref=dst, send_sem=ssem, recv_sem=rsem, device_id=partner, device_id_type=MESH
-        )
-
-    if cores > 1:
-        w_copy = swap_of(w_src, w_recv, pair_sem.at[0], pair_sem.at[1])
-        w_copy.start()
 
     flat_dims = dims[0] + dims[1] + dims[2]
     weights = []
@@ -220,11 +200,40 @@
                             - f_bufs[k][1, t, :, cs] * a_bufs[k][1, t, :, cs]
                         )
 
+    for k in range(min(PRE, groups)):
+        build(k)
+
+    pl.semaphore_wait(barrier, devices - 1)
+
+    def share(src, dst, sems):
+        for j in others:
+            pltpu.make_async_remote_copy(
+                src_ref=src, dst_ref=dst.at[j - 1], send_sem=side_sem.at[sems], recv_sem=side_sem.at[sems + 1],
+                device_id=other[j], device_id_type=MESH,
+            ).start()
+        return pltpu.make_async_remote_copy(
+            src_ref=dst, dst_ref=dst, send_sem=side_sem.at[sems], recv_sem=side_sem.at[sems + 1],
+            device_id=other[others[0]], device_id_type=MESH,
+        )
+
+    f_copy = share(f_src, f_recv, 3)
+    partner = at(move(dims[3], 1)) if cores > 1 else None
+
+    def swap_of(src, dst, ssem, rsem):
+        return pltpu.make_async_remote_copy(
+            src_ref=src, dst_ref=dst, send_sem=ssem, recv_sem=rsem, device_id=partner, device_id_type=MESH
+        )
+
+    if cores > 1:
+        w_copy = swap_of(w_src, w_recv, pair_sem.at[0], pair_sem.at[1])
+        w_copy.start()
+
     def swap(piece):
         return swap_of(away.at[piece], r0.at[piece], pair_sem.at[2], swap_sem.at[piece])
 
     for k in range(groups):
-        build(k)
+        if k >= PRE:
+            build(k)
         for piece in range(k * parts, (k + 1) * parts):
             if cores > 1 and piece < EARLY:
                 swap(piece).start()
@@ -279,6 +288,11 @@
         for j in range(radix(step) - 1):
             value = value + recv[piece, base + j * span : base + (j + 1) * span]
         return value
+
+    if DELAY:
+        @pl.when(c_me == 1)
+        def _():
+            pl.delay(DELAY)
 
     squares = jnp.zeros((SUB, LANES), jnp.float32)
     for piece, s in schedule(orders):

time: 40.9 us -> 37.2 us (0.910)
  Pallas kernels: 38.7 us -> 35 us
    pallas_call x1, Pallas kernels: 38.7 us -> 35 us  [per_device(): pl.pallas_call(functools.partial(kernel, sizes, orders), out_shape=(pltpu...]
where the time goes in v2:
time: 37.2 us; the launch traced here: 37 us
  Pallas kernels  35 us (94%)
  between operations  1.3 us (3%)
  other arithmetic  0.7 us (2%)
    pallas_call x1, Pallas kernels, per_device(): pl.pallas_call(functools.partial(kernel, sizes, orders), out_shape=(pltpu...  35 us

profile of v2, /device:TPU:0, one launch (start us, length us, event | category | flops | bytes accessed | tf_op | source)
XLA Modules:
  0.0 37.0 jit_solution(10945929602143621683)
XLA Ops:
  1.3 35.0 %assemble.1 = (f32[32,1024]{1,0:T(8,128)S(1)}, f32[1,128]{1,0:T(1,128)S(1)}) custom-call(f32[1]{0:T(128)S(6)} %copy.8.target, s32[1]{0:T(128)S(6)} %copy.9.wl_index, s32[32]{0:T(128)} %tiles_in.1, f32[2,1024]{1,0:T(2,128)} %mode_in.1, f32[32,1024]{1,0:T(8,128)} %density_in.1, f32[2,32,4,8,1024]{4,3,2,1,0:T(8,128)} %bitcast.5, f32[2,32,4,8,1024]{4,3,2,1,0:T(8,128)} %bitcast.6), custom_call_target="tpu_custom_call" | custom-call | tf_op jit(solution)/shard_map/assemble/pallas_call | solution.py:363
  36.3 0.7 %broadcast_divide_fusion = f32[32,1024]{1,0:T(8,128)} fusion(f32[32,1024]{1,0:T(8,128)S(1)} %get-tuple-element.7, f32[]{:T(128)S(1)} %bitcast.4), kind=kLoop, calls=%fused_computation | loop fusion | flops 32768 | bytes 262148 | tf_op jit(solution)/shard_map/div | solution.py:396

commit v3 on v2

--- a/solution.py
+++ b/solution.py
@@ -14,10 +14,8 @@
 PATTERNS = ('B.z.w.A', 'A.B.zw', 'w.A.z.B', 'B.w.A.z', 'A.z.B.w', 'A.B.w.z', 'A.w.z.B', 'A.B.zw', 'z.A.B.w', 'B.A.z.w', 'B.z.A.w', 'z.B.A.w', 'B.w.A.z', 'w.A.B.z', 'A.B.zw', 'B.A.zw')
 SPACE = 0.3
 LAG = 4.0
-EARLY = 16
-PRE = 0
 DELAY = 2000
-FIRST = 1
+EAGER = 2
 ORDER = ((0, -1), (1, -1), (2, -1), (3, -1), (4, -1), (5, -1), (6, -1), (7, -1), (8, -1), (9, -1), (10, -1), (11, -1), (12, -1), (13, -1), (14, -1), (15, -1), (0, 0), (1, 0), (2, 0), (3, 0), (4, 0), (5, 0), (6, 0), (7, 0), (8, 0), (9, 0), (10, 0), (11, 0), (12, 0), (13, 0), (14, 0), (15, 0), (0, 1), (1, 1), (2, 1), (3, 1), (4, 1), (5, 1), (6, 1), (7, 1), (8, 1), (9, 1), (10, 1), (11, 1), (12, 1), (13, 1), (14, 1), (15, 1), (0, 2), (1, 2), (2, 2), (3, 2), (4, 2), (5, 2), (6, 2), (8, 2), (9, 2), (10, 2), (11, 2), (12, 2), (13, 2), (0, 3), (2, 3), (3, 3), (4, 3), (12, 3), (13, 3), (6, 3), (8, 3), (7, 2), (9, 3), (5, 3), (14, 2), (15, 2), (10, 3), (11, 3))
 
 
@@ -64,7 +62,7 @@
 
 def kernel(
     sizes, orders, target, wl_index, tiles_in, mode_in, density_in, fwd, adj, shaped_out, norm_out,
-    tile_of, mode, density, line, f_src, f_recv, w_src, w_recv, q_src, q_recv, slope, own, away, r0, recv,
+    tile_of, mode, density, line, f_src, f_recv, w_src, w_recv, q_src, q_recv, slope, own, away, r0, recv, raw,
     in_sem, side_sem, pair_sem, swap_sem, step_sem, *bufs,
 ):
     g1, g2, cores, deep, groups, parts, rows, cols = sizes
@@ -131,13 +129,13 @@
             pltpu.make_async_copy(adj.at[:, :, k], a_bufs[k], in_sem.at[2 * k + 1]),
         )
         loads.append(pair)
-    for pair in loads[:FIRST]:
+    for pair in loads[:1]:
         for copy in pair:
             copy.start()
 
     line_copy.wait()
     mode_copy.wait()
-    for pair in loads[FIRST:]:
+    for pair in loads[1:]:
         for copy in pair:
             copy.start()
     density_copy.start()
@@ -200,9 +198,6 @@
                             - f_bufs[k][1, t, :, cs] * a_bufs[k][1, t, :, cs]
                         )
 
-    for k in range(min(PRE, groups)):
-        build(k)
-
     pl.semaphore_wait(barrier, devices - 1)
 
     def share(src, dst, sems):
@@ -218,6 +213,11 @@
 
     f_copy = share(f_src, f_recv, 3)
     partner = at(move(dims[3], 1)) if cores > 1 else None
+    eager = range(min(EAGER, parts)) if cores == 2 and per_core > 1 else range(0)
+    links = [(e, j, h) for e in eager for h in range(2) for j in range(1, radix(orders[e][0]))]
+
+    def across(e, j, h):
+        return at(move(list(orders[e][0]) + dims[3] * h, j + h * radix(orders[e][0])))
 
     def swap_of(src, dst, ssem, rsem):
         return pltpu.make_async_remote_copy(
@@ -225,26 +225,54 @@
         )
 
     if cores > 1:
-        w_copy = swap_of(w_src, w_recv, pair_sem.at[0], pair_sem.at[1])
-        w_copy.start()
+        for n, where in enumerate([partner] + [across(*link) for link in links]):
+            pltpu.make_async_remote_copy(
+                src_ref=w_src, dst_ref=w_recv.at[n], send_sem=pair_sem.at[0], recv_sem=pair_sem.at[1],
+                device_id=where, device_id_type=MESH,
+            ).start()
+        w_copy = swap_of(w_recv, w_recv, pair_sem.at[0], pair_sem.at[1])
+
+    def kept(piece):
+        return per_core // radix(orders[piece][0]) if piece in eager else per_core
 
     def swap(piece):
-        return swap_of(away.at[piece], r0.at[piece], pair_sem.at[2], swap_sem.at[piece])
+        part = pl.ds(0, kept(piece))
+        return swap_of(away.at[piece, part], r0.at[piece, part], pair_sem.at[2], swap_sem.at[piece])
+
+    def swapped(k):
+        part = pl.ds(k * parts, parts)
+        return swap_of(away.at[part], r0.at[part], pair_sem.at[2], swap_sem.at[parts - 1 + k])
+
+    def group_swap(piece):
+        return swap_of(away.at[piece], r0.at[piece], pair_sem.at[2], swap_sem.at[parts - 1 + piece // parts])
+
+    def swap_out(piece):
+        (swap(piece) if piece < parts else group_swap(piece)).start()
+
+    def send_raw(e):
+        step, span = orders[e][0], kept(e)
+        for h, src in enumerate((own, away)):
+            for j in range(1, radix(step)):
+                pltpu.make_async_remote_copy(
+                    src_ref=src.at[e, pl.ds(j * span, span)],
+                    dst_ref=raw.at[e, h, pl.ds((j - 1) * span, span)],
+                    send_sem=pair_sem.at[2 + (h == 0)], recv_sem=step_sem.at[e, 0],
+                    device_id=across(e, j, h), device_id_type=MESH,
+                ).start()
 
     for k in range(groups):
-        if k >= PRE:
-            build(k)
+        build(k)
         for piece in range(k * parts, (k + 1) * parts):
-            if cores > 1 and piece < EARLY:
-                swap(piece).start()
+            if piece in eager:
+                send_raw(piece)
+        for piece in range(k * parts, (k + 1) * parts):
+            if cores > 1:
+                swap_out(piece)
 
     density_copy.wait()
     slope[...] = 4.0 * (1.0 - jnp.tanh(4.0 * (density[...] - 0.5)) ** 2)
 
     f_copy.wait_recv()
-    for piece in range(EARLY, pieces):
-        if cores > 1:
-            swap(piece).start()
     total_fom = fom + jnp.sum(f_recv[...], axis=0)
     scale = total_fom / devices + 1.0
 
@@ -254,7 +282,10 @@
     factor = wide_factor(aim, part)
     if cores > 1:
         w_copy.wait_recv()
-        other_factor = wide_factor(w_recv[0:1, :], w_recv[1:2, :])
+        other_factor, *link_factors = [
+            wide_factor(w_recv[n, 0:1, :], w_recv[n, 1:2, :]) for n in range(1 + len(links))
+        ]
+        link_factor = dict(zip(links, link_factors))
 
     spans, bases = [], []
     for steps in orders:
@@ -279,6 +310,17 @@
 
     def take(piece, s):
         step, span, base = orders[piece][s], spans[piece][s], bases[piece][s]
+        if s == 0 and piece in eager:
+            got = raw.at[piece, :, pl.ds(0, (radix(step) - 1) * span)]
+            pltpu.make_async_remote_copy(
+                src_ref=got, dst_ref=got, send_sem=pair_sem.at[3], recv_sem=step_sem.at[piece, 0],
+                device_id=at(move(step, 1)), device_id_type=MESH,
+            ).wait_recv()
+            value = own[piece, :span]
+            for h in range(2):
+                for j in range(1, radix(step)):
+                    value = value + raw[piece, h, (j - 1) * span : j * span] * link_factor[piece, j, h]
+            return value
         got = recv.at[piece, pl.ds(base, (radix(step) - 1) * span)]
         pltpu.make_async_remote_copy(
             src_ref=got, dst_ref=got, send_sem=pair_sem.at[3], recv_sem=step_sem.at[piece, s],
@@ -295,15 +337,21 @@
             pl.delay(DELAY)
 
     squares = jnp.zeros((SUB, LANES), jnp.float32)
+    opened = set()
     for piece, s in schedule(orders):
         steps = orders[piece]
         if s < 0:
             if cores > 1:
-                swap(piece).wait_recv()
-                own[piece] = own[piece] * factor + r0[piece] * other_factor
+                if piece < parts:
+                    swap(piece).wait_recv()
+                elif piece // parts not in opened:
+                    opened.add(piece // parts)
+                    swapped(piece // parts).wait_recv()
+                part = slice(0, kept(piece))
+                own[piece, part] = own[piece, part] * factor + r0[piece, part] * other_factor
             else:
                 own[piece] = own[piece] * factor
-            if steps:
+            if steps and piece not in eager:
                 start(piece, 0)
         elif s < len(steps) - 1:
             own[piece, : spans[piece][s]] = take(piece, s)
@@ -350,6 +398,8 @@
     per_core = g1 * g2 * deep
     dims = [digits_of(0, g1), digits_of(1, g2), digits_of(2, deep)]
     orders = [steps_of(PATTERNS[i % len(PATTERNS)], dims) for i in range(pieces)]
+    eager = orders[: min(EAGER, parts)] if cores == 2 and per_core > 1 else []
+    messages = 1 + sum(2 * (radix(steps[0]) - 1) for steps in eager)
     fwd = forward.reshape(2, devices, groups, SUB, cols)
     adj = adjoint.reshape(2, devices, groups, SUB, cols)
     f32 = jnp.float32
@@ -373,7 +423,7 @@
             pltpu.VMEM((1, LANES), f32),
             pltpu.VMEM((peers, 1, LANES), f32),
             pltpu.VMEM((2, LANES), f32),
-            pltpu.VMEM((2, LANES), f32),
+            pltpu.VMEM((messages, 2, LANES), f32),
             pltpu.VMEM((1, LANES), f32),
             pltpu.VMEM((peers, 1, LANES), f32),
             pltpu.VMEM((tile_rows, cols), f32),
@@ -381,10 +431,11 @@
             block(per_core),
             block(per_core),
             block(per_core),
+            pltpu.VMEM((max(EAGER, 1), 2, per_core, SUB, width), f32),
             dma((2 * groups + 1,)),
             dma((7,)),
             dma((4,)),
-            dma((pieces,)),
+            dma((parts + groups - 1,)),
             dma((pieces, max(len(o) for o in orders))),
         ]
         + [pltpu.VMEM((2, devices, SUB, cols), f32)] * (2 * groups),

time: 37.2 us -> 36.4 us (0.978)
  Pallas kernels: 35 us -> 34.2 us
    pallas_call x1, Pallas kernels: 35 us -> 34.2 us  [per_device(): pl.pallas_call(functools.partial(kernel, sizes, orders), out_shape=(pltpu...]
where the time goes in v3:
time: 36.4 us; the launch traced here: 36.2 us
  Pallas kernels  34.2 us (94%)
  between operations  1.3 us (4%)
  other arithmetic  0.7 us (2%)
    pallas_call x1, Pallas kernels, per_device(): pl.pallas_call(functools.partial(kernel, sizes, orders), out_shape=(pltpu...  34.2 us

profile of v3, /device:TPU:0, one launch (start us, length us, event | category | flops | bytes accessed | tf_op | source)
XLA Modules:
  0.0 36.2 jit_solution(12144605432308034735)
XLA Ops:
  1.3 34.2 %assemble.1 = (f32[32,1024]{1,0:T(8,128)S(1)}, f32[1,128]{1,0:T(1,128)S(1)}) custom-call(f32[1]{0:T(128)S(6)} %copy.8.target, s32[1]{0:T(128)S(6)} %copy.9.wl_index, s32[32]{0:T(128)} %tiles_in.1, f32[2,1024]{1,0:T(2,128)} %mode_in.1, f32[32,1024]{1,0:T(8,128)} %density_in.1, f32[2,32,4,8,1024]{4,3,2,1,0:T(8,128)} %bitcast.5, f32[2,32,4,8,1024]{4,3,2,1,0:T(8,128)} %bitcast.6), custom_call_target="tpu_custom_call" | custom-call | tf_op jit(solution)/shard_map/assemble/pallas_call | solution.py:413
  35.5 0.7 %broadcast_divide_fusion = f32[32,1024]{1,0:T(8,128)} fusion(f32[32,1024]{1,0:T(8,128)S(1)} %get-tuple-element.7, f32[]{:T(128)S(1)} %bitcast.4), kind=kLoop, calls=%fused_computation | loop fusion | flops 32768 | bytes 262148 | tf_op jit(solution)/shard_map/div | solution.py:447

commit v4 on v3

--- a/solution.py
+++ b/solution.py
@@ -11,12 +11,12 @@
 SUB = 8
 LANES = 128
 PIECES = 16
-PATTERNS = ('B.z.w.A', 'A.B.zw', 'w.A.z.B', 'B.w.A.z', 'A.z.B.w', 'A.B.w.z', 'A.w.z.B', 'A.B.zw', 'z.A.B.w', 'B.A.z.w', 'B.z.A.w', 'z.B.A.w', 'B.w.A.z', 'w.A.B.z', 'A.B.zw', 'B.A.zw')
+PATTERNS = ('Az.B.w', 'B.w.A.z', 'z.B.A.w', 'B.A.z.w', 'A.w.B.z', 'A.w.B.z', 'B.A.zw', 'B.A.zw', 'z.B.A.w', 'A.Bz.w', 'B.w.Az', 'B.A.zw', 'A.B.zw', 'A.Bz.w', 'w.A.Bz', 'z.AB.w')
 SPACE = 0.3
 LAG = 4.0
-DELAY = 2000
+DELAY = 2800
 EAGER = 2
-ORDER = ((0, -1), (1, -1), (2, -1), (3, -1), (4, -1), (5, -1), (6, -1), (7, -1), (8, -1), (9, -1), (10, -1), (11, -1), (12, -1), (13, -1), (14, -1), (15, -1), (0, 0), (1, 0), (2, 0), (3, 0), (4, 0), (5, 0), (6, 0), (7, 0), (8, 0), (9, 0), (10, 0), (11, 0), (12, 0), (13, 0), (14, 0), (15, 0), (0, 1), (1, 1), (2, 1), (3, 1), (4, 1), (5, 1), (6, 1), (7, 1), (8, 1), (9, 1), (10, 1), (11, 1), (12, 1), (13, 1), (14, 1), (15, 1), (0, 2), (1, 2), (2, 2), (3, 2), (4, 2), (5, 2), (6, 2), (8, 2), (9, 2), (10, 2), (11, 2), (12, 2), (13, 2), (0, 3), (2, 3), (3, 3), (4, 3), (12, 3), (13, 3), (6, 3), (8, 3), (7, 2), (9, 3), (5, 3), (14, 2), (15, 2), (10, 3), (11, 3))
+ORDER = ((0, -1), (1, -1), (2, -1), (3, -1), (4, -1), (5, -1), (6, -1), (7, -1), (8, -1), (9, -1), (10, -1), (11, -1), (12, -1), (13, -1), (14, -1), (15, -1), (0, 0), (1, 0), (2, 0), (3, 0), (4, 0), (5, 0), (6, 0), (7, 0), (8, 0), (9, 0), (10, 0), (11, 0), (12, 0), (13, 0), (14, 0), (15, 0), (0, 1), (1, 1), (2, 1), (3, 1), (4, 1), (5, 1), (6, 1), (7, 1), (8, 1), (9, 1), (10, 1), (11, 1), (12, 1), (13, 1), (14, 1), (15, 1), (1, 2), (2, 2), (3, 2), (4, 2), (5, 2), (8, 2), (9, 2), (10, 2), (14, 2), (15, 2), (1, 3), (4, 3), (11, 2), (7, 2), (0, 2), (5, 3), (6, 2), (12, 2), (13, 2), (3, 3), (2, 3), (8, 3))
 
 
 def plane(wide):
@@ -150,6 +150,10 @@
     w_src[0:1, :] = jnp.full((1, LANES), aim)
     w_src[1:2, :] = part
 
+    sem_of = {}
+    for piece, steps in enumerate(orders):
+        for s in range(len(steps)):
+            sem_of[piece, s] = len(sem_of)
     flat_dims = dims[0] + dims[1] + dims[2]
     weights = []
     for steps in orders:
@@ -256,7 +260,7 @@
                 pltpu.make_async_remote_copy(
                     src_ref=src.at[e, pl.ds(j * span, span)],
                     dst_ref=raw.at[e, h, pl.ds((j - 1) * span, span)],
-                    send_sem=pair_sem.at[2 + (h == 0)], recv_sem=step_sem.at[e, 0],
+                    send_sem=pair_sem.at[2 + (h == 0)], recv_sem=step_sem.at[sem_of[e, 0]],
                     device_id=across(e, j, h), device_id_type=MESH,
                 ).start()
 
@@ -304,7 +308,7 @@
             pltpu.make_async_remote_copy(
                 src_ref=own.at[piece, pl.ds(j * span, span)],
                 dst_ref=recv.at[piece, pl.ds(base + (j - 1) * span, span)],
-                send_sem=pair_sem.at[3], recv_sem=step_sem.at[piece, s],
+                send_sem=pair_sem.at[3], recv_sem=step_sem.at[sem_of[piece, s]],
                 device_id=at(move(step, j)), device_id_type=MESH,
             ).start()
 
@@ -313,7 +317,7 @@
         if s == 0 and piece in eager:
             got = raw.at[piece, :, pl.ds(0, (radix(step) - 1) * span)]
             pltpu.make_async_remote_copy(
-                src_ref=got, dst_ref=got, send_sem=pair_sem.at[3], recv_sem=step_sem.at[piece, 0],
+                src_ref=got, dst_ref=got, send_sem=pair_sem.at[3], recv_sem=step_sem.at[sem_of[piece, 0]],
                 device_id=at(move(step, 1)), device_id_type=MESH,
             ).wait_recv()
             value = own[piece, :span]
@@ -323,7 +327,7 @@
             return value
         got = recv.at[piece, pl.ds(base, (radix(step) - 1) * span)]
         pltpu.make_async_remote_copy(
-            src_ref=got, dst_ref=got, send_sem=pair_sem.at[3], recv_sem=step_sem.at[piece, s],
+            src_ref=got, dst_ref=got, send_sem=pair_sem.at[3], recv_sem=step_sem.at[sem_of[piece, s]],
             device_id=at(move(step, 1)), device_id_type=MESH,
         ).wait_recv()
         value = own[piece, :span]
@@ -436,7 +440,7 @@
             dma((7,)),
             dma((4,)),
             dma((parts + groups - 1,)),
-            dma((pieces, max(len(o) for o in orders))),
+            dma((max(sum(len(steps) for steps in orders), 1),)),
         ]
         + [pltpu.VMEM((2, devices, SUB, cols), f32)] * (2 * groups),
         compiler_params=pltpu.CompilerParams(

time: 36.4 us -> 35.8 us (0.984)
  Pallas kernels: 34.2 us -> 33.6 us
    pallas_call x1, Pallas kernels: 34.2 us -> 33.6 us  [per_device(): pl.pallas_call(functools.partial(kernel, sizes, orders), out_shape=(pltpu...]
where the time goes in v4:
time: 35.8 us; the launch traced here: 35.6 us
  Pallas kernels  33.6 us (94%)
  between operations  1.3 us (4%)
  other arithmetic  0.7 us (2%)
    pallas_call x1, Pallas kernels, per_device(): pl.pallas_call(functools.partial(kernel, sizes, orders), out_shape=(pltpu...  33.6 us

profile of v4, /device:TPU:0, one launch (start us, length us, event | category | flops | bytes accessed | tf_op | source)
XLA Modules:
  0.0 35.6 jit_solution(243128081268867631)
XLA Ops:
  1.3 33.6 %assemble.1 = (f32[32,1024]{1,0:T(8,128)S(1)}, f32[1,128]{1,0:T(1,128)S(1)}) custom-call(f32[1]{0:T(128)S(6)} %copy.8.target, s32[1]{0:T(128)S(6)} %copy.9.wl_index, s32[32]{0:T(128)} %tiles_in.1, f32[2,1024]{1,0:T(2,128)} %mode_in.1, f32[32,1024]{1,0:T(8,128)} %density_in.1, f32[2,32,4,8,1024]{4,3,2,1,0:T(8,128)} %bitcast.5, f32[2,32,4,8,1024]{4,3,2,1,0:T(8,128)} %bitcast.6), custom_call_target="tpu_custom_call" | custom-call | tf_op jit(solution)/shard_map/assemble/pallas_call | solution.py:417
  34.9 0.7 %broadcast_divide_fusion = f32[32,1024]{1,0:T(8,128)} fusion(f32[32,1024]{1,0:T(8,128)S(1)} %get-tuple-element.7, f32[]{:T(128)S(1)} %bitcast.4), kind=kLoop, calls=%fused_computation | loop fusion | flops 32768 | bytes 262148 | tf_op jit(solution)/shard_map/div | solution.py:451

commit v5 on v4

--- a/solution.py
+++ b/solution.py
@@ -171,9 +171,7 @@
 
     tile_copy.wait()
 
-    def build(k):
-        for copy in loads[k]:
-            copy.wait()
+    def build(k, some):
         for half in range(cores):
 
             @pl.loop(0, g1 * g2)
@@ -192,7 +190,7 @@
                         if o:
                             there = shift(there, d, o)
                     t = tile_of[flat(there)]
-                    for p in range(parts):
+                    for p in some:
                         cs = slice(p * width, (p + 1) * width)
                         piece = k * parts + p
                         kind = kind_of[piece]
@@ -265,10 +263,16 @@
                 ).start()
 
     for k in range(groups):
-        build(k)
+        for copy in loads[k]:
+            copy.wait()
+        first = len(eager) if k == 0 else 0
+        if first:
+            build(k, range(first))
         for piece in range(k * parts, (k + 1) * parts):
             if piece in eager:
                 send_raw(piece)
+        if first < parts:
+            build(k, range(first, parts))
         for piece in range(k * parts, (k + 1) * parts):
             if cores > 1:
                 swap_out(piece)

time: 35.8 us -> 36 us (level)
  no operation moved by 1% of the time
where the time goes in v5:
time: 36 us; the launch traced here: 35.8 us
  Pallas kernels  33.8 us (94%)
  between operations  1.3 us (4%)
  other arithmetic  0.7 us (2%)
    pallas_call x1, Pallas kernels, per_device(): pl.pallas_call(functools.partial(kernel, sizes, orders), out_shape=(pltpu...  33.8 us

profile of v5, /device:TPU:0, one launch (start us, length us, event | category | flops | bytes accessed | tf_op | source)
XLA Modules:
  0.0 35.8 jit_solution(1512969710881170800)
XLA Ops:
  1.3 33.8 %assemble.1 = (f32[32,1024]{1,0:T(8,128)S(1)}, f32[1,128]{1,0:T(1,128)S(1)}) custom-call(f32[1]{0:T(128)S(6)} %copy.8.target, s32[1]{0:T(128)S(6)} %copy.9.wl_index, s32[32]{0:T(128)} %tiles_in.1, f32[2,1024]{1,0:T(2,128)} %mode_in.1, f32[32,1024]{1,0:T(8,128)} %density_in.1, f32[2,32,4,8,1024]{4,3,2,1,0:T(8,128)} %bitcast.5, f32[2,32,4,8,1024]{4,3,2,1,0:T(8,128)} %bitcast.6), custom_call_target="tpu_custom_call" | custom-call | tf_op jit(solution)/shard_map/assemble/pallas_call | solution.py:421
  35.1 0.7 %broadcast_divide_fusion = f32[32,1024]{1,0:T(8,128)} fusion(f32[32,1024]{1,0:T(8,128)S(1)} %get-tuple-element.7, f32[]{:T(128)S(1)} %bitcast.4), kind=kLoop, calls=%fused_computation | loop fusion | flops 32768 | bytes 262148 | tf_op jit(solution)/shard_map/div | solution.py:455
